TPU v7x, 128 devices: a whole 4x4x4 slice. The times are simulated.
128 devices in a mesh: leaf: 32 (over x, y, core), nbr: 4 (over z).
Axes of the slice: x: 4, y: 4, z: 4, core: 2. Of those that a mesh axis runs over, the one named last changes fastest.
Arguments:
- points: bfloat16 [1024, 32, 512], P('leaf'), may hold values from -1.1953125 to 1.1953125
- charges: bfloat16 [1024, 64, 512], P('leaf'), may hold values from -1.5 to 1.5
- projection: bfloat16 [1024, 256, 512], P('leaf', 'nbr'), may hold values from -0.25 to 0.25
- skeleton_index: int32 [1024, 256], P('leaf'), may hold values from 0 to 511, as said below
- near_ids: int32 [1024, 8], P('leaf', 'nbr'), may hold values from 0 to 1023, as said below
- far_ids: int32 [1024, 16], P('leaf', 'nbr'), may hold values from 0 to 1023, as said below
Outputs:
- potentials: float32 [1024, 64, 512], P('leaf', None, 'nbr')
Inputs may be any that keep to these rules, and one draw needn't show every extreme that they name: `skeleton_index`: each row holds 256 different point numbers of its leaf. `near_ids`: take the rows of one block of 32 leaves (leaf numbers k * 32 to k * 32 + 31) and one of the 4 equal groups of columns: at most 3 of its entries name leaves of any one such block, and some block is named exactly 3 times. `far_ids`: take the rows of one block of 32 leaves and one of the 4 equal groups of columns: at most 5 of its entries name leaves of any one such block, and some block is named exactly 5 times.
All inputs are finite; a program needn't handle non-finite values.
Results may differ from a plain program's by a relative error of at most 0.002.
Values may be sent and summed in bfloat16 or wider, within the bound.
A program may use at most 128 MiB of HBM per device.

v0:
```python
import math
import jax
import jax.numpy as jnp
from jax import lax
from jax.sharding import PartitionSpec as P

GAMMA = 1.0


def kernel_terms(targets, sources, weights):
    target_f32 = targets.astype(jnp.float32)
    source_f32 = sources.astype(jnp.float32)
    inner_terms = jnp.einsum("dt,dm->tm", targets, sources, preferred_element_type=jnp.float32)
    distance = (
        jnp.sum(target_f32 * target_f32, axis=0)[:, None]
        + jnp.sum(source_f32 * source_f32, axis=0)[None, :]
        - 2.0 * inner_terms
    )
    kernel = jnp.exp(-GAMMA * distance)
    return jnp.einsum(
        "rm,tm->rt",
        weights.astype(jnp.float32),
        kernel,
        precision=lax.Precision.HIGHEST,
        preferred_element_type=jnp.float32,
    )


def group_terms(targets, sources, weights):
    item_count = targets.shape[0]
    column_count = sources.shape[2]
    block_rows = math.gcd(item_count, max(1, 8192 // column_count))
    steps_count = item_count // block_rows

    def run_block(batch_rows):
        return jax.vmap(kernel_terms)(batch_rows[0], batch_rows[1], batch_rows[2])

    stacked = (
        targets.reshape((steps_count, block_rows) + targets.shape[1:]),
        sources.reshape((steps_count, block_rows) + sources.shape[1:]),
        weights.reshape((steps_count, block_rows) + weights.shape[1:]),
    )
    result = lax.map(run_block, stacked)
    return result.reshape((item_count,) + result.shape[2:])


def slot_plan(id_block, capacity, groups, leaf_dev):
    flat_ids = id_block.reshape(-1)
    owners = flat_ids // leaf_dev
    local_leaf = flat_ids % leaf_dev
    member = (owners[:, None] == jnp.arange(groups, dtype=jnp.int32)[None, :]).astype(jnp.int32)
    before = jnp.cumsum(member, axis=0) - member
    rank_slot = jnp.sum(before * member, axis=1)
    return (local_leaf, owners * capacity + rank_slot)


def slot_table(values, slot_ids, capacity, groups):
    matches = slot_ids[:, None] == jnp.arange(groups * capacity, dtype=jnp.int32)[None, :]
    return jnp.sum(jnp.where(matches, values[:, None], 0), axis=0).reshape(groups, capacity)


def gather_entries(received, slot_ids, leaf_dev):
    flat_rows = received.reshape((-1,) + received.shape[2:])
    picked = flat_rows[slot_ids]
    per_target = slot_ids.shape[0] // leaf_dev
    picked = picked.reshape(leaf_dev, per_target, picked.shape[1], picked.shape[2])
    return picked.transpose(0, 2, 1, 3).reshape(
        leaf_dev, picked.shape[2], per_target * picked.shape[3]
    )


def per_device(points, charges, projection, skeleton_index, near_ids, far_ids):
    leaf_dev = points.shape[0]
    groups = lax.axis_size("leaf")
    near_dev = near_ids.shape[1]
    far_dev = far_ids.shape[1]
    cap_near = max(2, (5 * leaf_dev * near_dev + 4 * groups - 1) // (4 * groups))
    cap_far = max(2, (5 * leaf_dev * far_dev + 4 * groups - 1) // (4 * groups))
    partial_value = jnp.einsum(
        "lrp,lsp->lrs", charges, projection, preferred_element_type=jnp.float32
    ).astype(jnp.bfloat16)
    skeleton_charges = lax.all_gather(partial_value, "nbr", axis=2, tiled=True)
    skeleton_points = jnp.take_along_axis(points, skeleton_index[:, None, :], axis=2)
    near_local, near_slots = slot_plan(near_ids, cap_near, groups, leaf_dev)
    far_local, far_slots = slot_plan(far_ids, cap_far, groups, leaf_dev)
    near_table = slot_table(near_local, near_slots, cap_near, groups)
    far_table = slot_table(far_local, far_slots, cap_far, groups)
    near_wanted, far_wanted = (
        lax.all_to_all(near_table, "leaf", split_axis=0, concat_axis=0, tiled=True),
        lax.all_to_all(far_table, "leaf", split_axis=0, concat_axis=0, tiled=True),
    )
    near_points, near_weights, far_points, far_weights = (
        lax.all_to_all(points[near_wanted], "leaf", split_axis=0, concat_axis=0, tiled=True),
        lax.all_to_all(charges[near_wanted], "leaf", split_axis=0, concat_axis=0, tiled=True),
        lax.all_to_all(
            skeleton_points[far_wanted], "leaf", split_axis=0, concat_axis=0, tiled=True
        ),
        lax.all_to_all(
            skeleton_charges[far_wanted], "leaf", split_axis=0, concat_axis=0, tiled=True
        ),
    )
    sources = jnp.concatenate(
        [
            gather_entries(near_points, near_slots, leaf_dev),
            gather_entries(far_points, far_slots, leaf_dev),
        ],
        axis=2,
    )
    weights = jnp.concatenate(
        [
            gather_entries(near_weights, near_slots, leaf_dev),
            gather_entries(far_weights, far_slots, leaf_dev),
        ],
        axis=2,
    )
    terms = group_terms(points, sources, weights)
    return lax.psum_scatter(terms, "nbr", scatter_dimension=2, tiled=True)


def solution(mesh):
    in_specs = (
        P("leaf", None, None),
        P("leaf", None, None),
        P("leaf", "nbr", None),
        P("leaf", None),
        P("leaf", "nbr"),
        P("leaf", "nbr"),
    )
    out_specs = P("leaf", None, "nbr")
    return jax.shard_map(
        per_device, mesh=mesh, in_specs=in_specs, out_specs=out_specs, check_vma=False
    )
```

profile of v0, /device:TPU:1, one launch (start us, length us, event | category | flops | bytes accessed | tf_op | source)
XLA Modules:
  0.0 669.3 jit_solution(7180529218226698054)
XLA Ops:
  8.9 8.6 %all-to-all-start.2 = ((s32[32,1,5]{2,1,0:T(1,128)}), s32[32,1,5]{2,1,0:T(1,128)S(1)}, u32[]{:S(2)}, u32[]{:S(2)}) async-start(s32[32,1,5]{2,1,0:T(1,128)} %bitcast.12), calls=%async_computation.2 | async-start | bytes 32768 | tf_op jit(solution)/shard_map/all_to_all | solution.py:90
  24.9 132.5 %gather_fusion.8 = bf16[8192,32]{1,0:T(8,128)(2,1)} fusion(bf16[32,32,512]{1,2,0:T(8,128)(2,1)} %copy.77, s32[8192]{0:T(1024)S(1)} %bitcast.83), kind=kCustom, calls=%fused_computation.8 | custom fusion | bytes 1114112 | tf_op jit(solution)/shard_map/jit(take_along_axis)/gather | solution.py:83
  162.6 7.3 %all-to-all-start = ((s32[32,1,3]{2,1,0:T(1,128)}), s32[32,1,3]{2,1,0:T(1,128)S(1)}, u32[]{:S(2)}, u32[]{:S(2)}) async-start(s32[32,1,3]{2,1,0:T(1,128)} %bitcast.4), calls=%async_computation | async-start | bytes 32768 | tf_op jit(solution)/shard_map/all_to_all | solution.py:89
  170.0 9.2 %gather_fusion.6 = bf16[160,32,256]{1,2,0:T(8,128)(2,1)} fusion(bf16[32,32,256]{1,2,0:T(8,128)(2,1)} %select_bitcast_fusion, s32[1024]{0:T(1024)S(1)} %pad_clamp_fusion.1), kind=kCustom, calls=%fused_computation.6 | custom fusion | bytes 5243520 | tf_op jit(solution)/shard_map/gather | solution.py:96
  179.1 9.8 %copy.78 = bf16[32,5,32,256]{3,2,1,0:T(8,128)(2,1)} copy(bf16[32,5,32,256]{2,3,1,0:T(8,128)(2,1)} %bitcast.89) | data formatting | bytes 5242880 | tf_op jit(solution)/shard_map/gather | solution.py:96
  188.9 7.6 %all-to-all-start.5 = ((bf16[32,5,32,256]{3,2,1,0:T(8,128)(2,1)}), bf16[32,5,32,256]{3,2,1,0:T(8,128)(2,1)}, u32[]{:S(2)}, u32[]{:S(2)}) async-start(bf16[32,5,32,256]{3,2,1,0:T(8,128)(2,1)} %copy.78), calls=%async_computation.5 | async-start | bytes 5242880 | tf_op jit(solution)/shard_map/all_to_all | solution.py:95
  199.4 31.1 %all-to-all-done.5 = bf16[32,5,32,256]{3,2,1,0:T(8,128)(2,1)} async-done(((bf16[32,5,32,256]{3,2,1,0:T(8,128)(2,1)}), bf16[32,5,32,256]{3,2,1,0:T(8,128)(2,1)}, u32[]{:S(2)}, u32[]{:S(2)}) %all-to-all-start.5) | async-done | bytes 2621472 | tf_op jit(solution)/shard_map/all_to_all | solution.py:95
  230.5 5.3 all-to-all-start.4
  235.8 6.0 gather_fusion
  241.8 33.9 %all-to-all-done.4 = bf16[32,3,32,512]{3,2,1,0:T(8,128)(2,1)} async-done(((bf16[32,3,32,512]{3,2,1,0:T(8,128)(2,1)}), bf16[32,3,32,512]{3,2,1,0:T(8,128)(2,1)}, u32[]{:S(2)}, u32[]{:S(2)}) %all-to-all-start.4) | async-done | bytes 3145760 | tf_op jit(solution)/shard_map/all_to_all | solution.py:93
  287.1 33.1 %all-gather.2.cloned.1.call-done = bf16[32,64,256]{1,0,2:T(8,128)(2,1)} async-done(((bf16[32,64,64]{1,0,2:T(8,128)(2,1)}), bf16[32,64,256]{1,0,2:T(8,128)(2,1)}) %all-gather.2.cloned.1.call-update) | async-done | bytes 1048592 | tf_op jit(solution)/shard_map/all_gather | solution.py:82
  323.0 7.7 %gather_fusion.2 = bf16[160,64,256]{2,1,0:T(8,128)(2,1)} fusion(bf16[32,64,256]{2,1,0:T(8,128)(2,1)S(1)} %copy.73, s32[1024]{0:T(1024)S(1)} %pad_clamp_fusion.1), kind=kCustom, calls=%fused_computation.2 | custom fusion | bytes 10486400 | tf_op jit(solution)/shard_map/gather | solution.py:99
  330.7 27.6 %all-to-all-done.1 = bf16[32,3,64,512]{3,2,1,0:T(8,128)(2,1)} async-done(((bf16[32,3,64,512]{3,2,1,0:T(8,128)(2,1)}), bf16[32,3,64,512]{3,2,1,0:T(8,128)(2,1)}, u32[]{:S(2)}, u32[]{:S(2)}) %all-to-all-start.1) | async-done | bytes 6291488 | tf_op jit(solution)/shard_map/all_to_all | solution.py:94
  358.3 14.0 %all-to-all-start.3 = ((bf16[32,5,64,256]{3,2,1,0:T(8,128)(2,1)}), bf16[32,5,64,256]{3,2,1,0:T(8,128)(2,1)}, u32[]{:S(2)}, u32[]{:S(2)}) async-start(bf16[32,5,64,256]{3,2,1,0:T(8,128)(2,1)} %bitcast.86), calls=%async_computation.3 | async-start | bytes 10485760 | tf_op jit(solution)/shard_map/all_to_all | solution.py:98
  397.6 5.7 gather_fusion.1
  403.3 8.5 %copy.69 = bf16[32,64,2,512]{3,2,1,0:T(2,128)(2,1)} copy(bf16[32,64,2,512]{3,1,2,0:T(8,128)(2,1)} %bitcast.87) | data formatting | bytes 8388608 | tf_op jit(solution)/shard_map/transpose | solution.py:67
  411.8 7.9 %concatenate.16 = bf16[8,4,64,1024]{3,2,1,0:T(8,128)(2,1)} reshape(bf16[32,64,2,512]{3,2,1,0:T(2,128)(2,1)} %copy.69) | data formatting | bytes 8388608 | tf_op jit(solution)/shard_map/concatenate | solution.py:109
  419.7 17.0 %all-to-all-done.3 = bf16[32,5,64,256]{3,2,1,0:T(8,128)(2,1)} async-done(((bf16[32,5,64,256]{3,2,1,0:T(8,128)(2,1)}), bf16[32,5,64,256]{3,2,1,0:T(8,128)(2,1)}, u32[]{:S(2)}, u32[]{:S(2)}) %all-to-all-start.3) | async-done | bytes 5242912 | tf_op jit(solution)/shard_map/all_to_all | solution.py:98
  436.7 5.2 gather_fusion.3
  441.9 8.1 %copy.75 = bf16[32,64,4,256]{3,2,1,0:T(4,128)(2,1)} copy(bf16[32,64,4,256]{3,1,2,0:T(8,128)(2,1)} %bitcast.88) | data formatting | bytes 8388608 | tf_op jit(solution)/shard_map/transpose | solution.py:67
  450.0 7.8 %concatenate.17 = bf16[8,4,64,1024]{3,2,1,0:T(8,128)(2,1)} reshape(bf16[32,64,4,256]{3,2,1,0:T(4,128)(2,1)} %copy.75) | data formatting | bytes 8388608 | tf_op jit(solution)/shard_map/concatenate | solution.py:109
  457.8 8.2 %pad_maximum_fusion = bf16[8,4,64,2048]{3,2,1,0:T(8,128)(2,1)} fusion(bf16[8,4,64,1024]{3,2,1,0:T(8,128)(2,1)} %concatenate.17, bf16[8,4,64,1024]{3,2,1,0:T(8,128)(2,1)} %concatenate.16), kind=kLoop, calls=%fused_computation.34 | loop fusion | flops 16777216 | bytes 16777216 | tf_op jit(solution)/shard_map/concatenate | solution.py:109
  465.9 146.8 %while.10 = (s32[]{:T(128)}, f32[8,4,64,512]{3,2,1,0:T(8,128)}, bf16[8,4,64,2048]{3,2,1,0:T(8,128)(2,1)}, bf16[8,4,32,512]{3,2,1,0:T(8,128)(2,1)S(1)}, bf16[8,4,32,2048]{3,2,1,0:T(8,128)(2,1)}, /*index=5*/s32[]{:T(128)}) while((s32[]{:T(128)}, f32[8,4,64,512]{3,2,1,0:T(8,128)}, bf16[8,4,64,2048]{3,2,1,0:T(8,128)(2,1)}, ...), condition=%wide.region_9.10_spmd, body=%wide.region_6.9_spmd.sunk | while | flops 3507410944 | bytes 36522060 | solution.py:43
  470.8 13.6 %fusion.45 = f32[8,4,64,512]{3,2,1,0:T(8,128)} fusion(f32[8,4,64,512]{3,2,1,0:T(8,128)} %get-tuple-element.85, s32[]{:T(128)} %get-tuple-element.84, f32[4,512,2048]{2,1,0:T(8,128)S(1)} %fusion.44, f32[4,2048]{1,0:T(4,128)S(1)} %multiply_reduce_fusion.4, f32[4,512]{1,0:T(4,128)S(1)} %multiply_reduce_fusion.5, ...), kind=kOutput, calls=%fused_computation.20.clone.1 | convolution fusion | flops 3238002688 | bytes 18392064 | tf_op jit(solution)/shard_map/while/body/eval_jaxpr/vmap(rm,tm->rt)/dot_general | solution.py:20
  489.2 13.6 %fusion.45 = f32[8,4,64,512]{3,2,1,0:T(8,128)} fusion(f32[8,4,64,512]{3,2,1,0:T(8,128)} %get-tuple-element.85, s32[]{:T(128)} %get-tuple-element.84, f32[4,512,2048]{2,1,0:T(8,128)S(1)} %fusion.44, f32[4,2048]{1,0:T(4,128)S(1)} %multiply_reduce_fusion.4, f32[4,512]{1,0:T(4,128)S(1)} %multiply_reduce_fusion.5, ...), kind=kOutput, calls=%fused_computation.20.clone.1 | convolution fusion | flops 3238002688 | bytes 18392064 | tf_op jit(solution)/shard_map/while/body/eval_jaxpr/vmap(rm,tm->rt)/dot_general | solution.py:20
  507.5 13.6 %fusion.45 = f32[8,4,64,512]{3,2,1,0:T(8,128)} fusion(f32[8,4,64,512]{3,2,1,0:T(8,128)} %get-tuple-element.85, s32[]{:T(128)} %get-tuple-element.84, f32[4,512,2048]{2,1,0:T(8,128)S(1)} %fusion.44, f32[4,2048]{1,0:T(4,128)S(1)} %multiply_reduce_fusion.4, f32[4,512]{1,0:T(4,128)S(1)} %multiply_reduce_fusion.5, ...), kind=kOutput, calls=%fused_computation.20.clone.1 | convolution fusion | flops 3238002688 | bytes 18392064 | tf_op jit(solution)/shard_map/while/body/eval_jaxpr/vmap(rm,tm->rt)/dot_general | solution.py:20
  525.8 13.6 %fusion.45 = f32[8,4,64,512]{3,2,1,0:T(8,128)} fusion(f32[8,4,64,512]{3,2,1,0:T(8,128)} %get-tuple-element.85, s32[]{:T(128)} %get-tuple-element.84, f32[4,512,2048]{2,1,0:T(8,128)S(1)} %fusion.44, f32[4,2048]{1,0:T(4,128)S(1)} %multiply_reduce_fusion.4, f32[4,512]{1,0:T(4,128)S(1)} %multiply_reduce_fusion.5, ...), kind=kOutput, calls=%fused_computation.20.clone.1 | convolution fusion | flops 3238002688 | bytes 18392064 | tf_op jit(solution)/shard_map/while/body/eval_jaxpr/vmap(rm,tm->rt)/dot_general | solution.py:20
  544.1 13.6 %fusion.45 = f32[8,4,64,512]{3,2,1,0:T(8,128)} fusion(f32[8,4,64,512]{3,2,1,0:T(8,128)} %get-tuple-element.85, s32[]{:T(128)} %get-tuple-element.84, f32[4,512,2048]{2,1,0:T(8,128)S(1)} %fusion.44, f32[4,2048]{1,0:T(4,128)S(1)} %multiply_reduce_fusion.4, f32[4,512]{1,0:T(4,128)S(1)} %multiply_reduce_fusion.5, ...), kind=kOutput, calls=%fused_computation.20.clone.1 | convolution fusion | flops 3238002688 | bytes 18392064 | tf_op jit(solution)/shard_map/while/body/eval_jaxpr/vmap(rm,tm->rt)/dot_general | solution.py:20
  562.4 13.6 %fusion.45 = f32[8,4,64,512]{3,2,1,0:T(8,128)} fusion(f32[8,4,64,512]{3,2,1,0:T(8,128)} %get-tuple-element.85, s32[]{:T(128)} %get-tuple-element.84, f32[4,512,2048]{2,1,0:T(8,128)S(1)} %fusion.44, f32[4,2048]{1,0:T(4,128)S(1)} %multiply_reduce_fusion.4, f32[4,512]{1,0:T(4,128)S(1)} %multiply_reduce_fusion.5, ...), kind=kOutput, calls=%fused_computation.20.clone.1 | convolution fusion | flops 3238002688 | bytes 18392064 | tf_op jit(solution)/shard_map/while/body/eval_jaxpr/vmap(rm,tm->rt)/dot_general | solution.py:20
  580.8 13.6 %fusion.45 = f32[8,4,64,512]{3,2,1,0:T(8,128)} fusion(f32[8,4,64,512]{3,2,1,0:T(8,128)} %get-tuple-element.85, s32[]{:T(128)} %get-tuple-element.84, f32[4,512,2048]{2,1,0:T(8,128)S(1)} %fusion.44, f32[4,2048]{1,0:T(4,128)S(1)} %multiply_reduce_fusion.4, f32[4,512]{1,0:T(4,128)S(1)} %multiply_reduce_fusion.5, ...), kind=kOutput, calls=%fused_computation.20.clone.1 | convolution fusion | flops 3238002688 | bytes 18392064 | tf_op jit(solution)/shard_map/while/body/eval_jaxpr/vmap(rm,tm->rt)/dot_general | solution.py:20
  599.1 13.6 %fusion.45 = f32[8,4,64,512]{3,2,1,0:T(8,128)} fusion(f32[8,4,64,512]{3,2,1,0:T(8,128)} %get-tuple-element.85, s32[]{:T(128)} %get-tuple-element.84, f32[4,512,2048]{2,1,0:T(8,128)S(1)} %fusion.44, f32[4,2048]{1,0:T(4,128)S(1)} %multiply_reduce_fusion.4, f32[4,512]{1,0:T(4,128)S(1)} %multiply_reduce_fusion.5, ...), kind=kOutput, calls=%fused_computation.20.clone.1 | convolution fusion | flops 3238002688 | bytes 18392064 | tf_op jit(solution)/shard_map/while/body/eval_jaxpr/vmap(rm,tm->rt)/dot_general | solution.py:20
  612.7 49.5 %reduce-scatter.2.cloned.1.call-done = f32[32,64,128]{2,1,0:T(8,128)} async-done(((f32[32,64,512]{2,1,0:T(8,128)}), f32[32,64,128]{2,1,0:T(8,128)}) %reduce-scatter.2.cloned.1.call-update) | async-done | bytes 1048592 | tf_op jit(solution)/shard_map/reduce_scatter | solution.py:117
  (88 shorter events, 94.8 us)
Async XLA Ops:
  6.5 229.3 %copy-start = (bf16[32,64,512]{2,1,0:T(8,128)(2,1)S(1)}, bf16[32,64,512]{2,1,0:T(8,128)(2,1)}, u32[]{:S(2)}) copy-start(bf16[32,64,512]{2,1,0:T(8,128)(2,1)} %param.9) | copy-start | bytes 6291460
  8.9 153.7 %all-to-all-start.2 = ((s32[32,1,5]{2,1,0:T(1,128)}), s32[32,1,5]{2,1,0:T(1,128)S(1)}, u32[]{:S(2)}, u32[]{:S(2)}) async-start(s32[32,1,5]{2,1,0:T(1,128)} %bitcast.12), calls=%async_computation.2 | async-start | bytes 32768 | tf_op jit(solution)/shard_map/all_to_all | solution.py:90
  162.6 26.4 %all-to-all-start = ((s32[32,1,3]{2,1,0:T(1,128)}), s32[32,1,3]{2,1,0:T(1,128)S(1)}, u32[]{:S(2)}, u32[]{:S(2)}) async-start(s32[32,1,3]{2,1,0:T(1,128)} %bitcast.4), calls=%async_computation | async-start | bytes 32768 | tf_op jit(solution)/shard_map/all_to_all | solution.py:89
  188.9 7.9 %copy-start.2 = (bf16[32,32,512]{2,1,0:T(8,128)(2,1)S(1)}, bf16[32,32,512]{2,1,0:T(8,128)(2,1)}, u32[]{:S(2)}) copy-start(bf16[32,32,512]{2,1,0:T(8,128)(2,1)} %param.8) | copy-start | bytes 3145732
  188.9 41.6 %all-to-all-start.5 = ((bf16[32,5,32,256]{3,2,1,0:T(8,128)(2,1)}), bf16[32,5,32,256]{3,2,1,0:T(8,128)(2,1)}, u32[]{:S(2)}, u32[]{:S(2)}) async-start(bf16[32,5,32,256]{3,2,1,0:T(8,128)(2,1)} %copy.78), calls=%async_computation.5 | async-start | bytes 5242880 | tf_op jit(solution)/shard_map/all_to_all | solution.py:95
  230.5 45.2 %all-to-all-start.4 = ((bf16[32,3,32,512]{3,2,1,0:T(8,128)(2,1)}), bf16[32,3,32,512]{3,2,1,0:T(8,128)(2,1)}, u32[]{:S(2)}, u32[]{:S(2)}) async-start(bf16[32,3,32,512]{3,2,1,0:T(8,128)(2,1)} %bitcast.90), calls=%async_computation.4 | async-start | bytes 6291456 | tf_op jit(solution)/shard_map/all_to_all | solution.py:93
  275.7 82.5 %all-to-all-start.1 = ((bf16[32,3,64,512]{3,2,1,0:T(8,128)(2,1)}), bf16[32,3,64,512]{3,2,1,0:T(8,128)(2,1)}, u32[]{:S(2)}, u32[]{:S(2)}) async-start(bf16[32,3,64,512]{3,2,1,0:T(8,128)(2,1)} %bitcast.85), calls=%async_computation.1 | async-start | bytes 12582912 | tf_op jit(solution)/shard_map/all_to_all | solution.py:94
  280.9 39.3 %all-gather.2.cloned.1.call-start = ((), (), s32[]{:S(2)}) async-start(), calls=%async_computation.7 | async-start | bytes 2621440 | tf_op jit(solution)/shard_map/all_gather | solution.py:82
  358.3 78.4 %all-to-all-start.3 = ((bf16[32,5,64,256]{3,2,1,0:T(8,128)(2,1)}), bf16[32,5,64,256]{3,2,1,0:T(8,128)(2,1)}, u32[]{:S(2)}, u32[]{:S(2)}) async-start(bf16[32,5,64,256]{3,2,1,0:T(8,128)(2,1)} %bitcast.86), calls=%async_computation.3 | async-start | bytes 10485760 | tf_op jit(solution)/shard_map/all_to_all | solution.py:98
  372.3 290.0 %reduce-scatter.2.cloned.1.call-start = ((), (), s32[]{:S(2)}) async-start(), calls=%async_computation.8 | async-start | bytes 5242880 | tf_op jit(solution)/shard_map/reduce_scatter | solution.py:117
  388.9 4.6 copy-start.3
  612.7 49.5 %copy-start.1 = (bf16[32,64,512]{2,1,0:T(8,128)(2,1)S(1)}, bf16[32,64,512]{2,1,0:T(8,128)(2,1)}, u32[]{:S(2)}) copy-start(bf16[32,64,512]{2,1,0:T(8,128)(2,1)} %param.9) | copy-start | bytes 6291460
Sparse Core Ops, SparseCore 0:
  287.2 32.9 all-gather.1
  612.9 49.3 reduce-scatter.1
where the time goes:
time: 679 us; the launch traced here: 669 us
  local copies, waits for them, and re-layouts  246 us (36%)
  waiting for transfers between devices  192 us (28%)
  matrix products  139 us (20%)
  starting transfers between devices  48.5 us (7%)
  other arithmetic  29.4 us (4%)
  between operations  13.9 us (2%)
    gather x1, local copies, waits for them, and re-layouts, per_device(): jnp.take_along_axis(points, skeleton_index[:, None, :], axis=2)  132 us
    dot_general x8, matrix products, kernel_terms(): jnp.einsum('rm,tm->rt', weights.astype(jnp.float32), kernel, precision=la...  109 us
    reduce_scatter x1, waiting for transfers between devices, per_device(): return lax.psum_scatter(terms, 'nbr', scatter_dimension=2, tiled=True)  49.5 us
    all_to_all x1, waiting for transfers between devices, per_device(): lax.all_to_all(points[near_wanted], 'leaf', split_axis=0, concat_axis=0,...  33.9 us
    all_gather x1, waiting for transfers between devices, per_device(): skeleton_charges = lax.all_gather(partial_value, 'nbr', axis=2, tiled=True)  33.1 us
    all_to_all x1, waiting for transfers between devices, per_device(): lax.all_to_all(skeleton_points[far_wanted], 'leaf', split_axis=0, concat_...  31.1 us
    all_to_all x1, waiting for transfers between devices, per_device(): lax.all_to_all(charges[near_wanted], 'leaf', split_axis=0, concat_axis=0,...  27.6 us
    dot_general x8, matrix products, kernel_terms(): jnp.einsum('dt,dm->tm', targets, sources, preferred_element_type=jnp.floa...  27.3 us
  transfers between devices with their start and end apart: 8, of which 6 were waited for; matrix products, arithmetic and copies ran while one was open for 35% of the time, Pallas kernels for 0%

commit v1 on v0

--- a/solution.py
+++ b/solution.py
@@ -79,7 +79,9 @@
     partial_value = jnp.einsum(
         "lrp,lsp->lrs", charges, projection, preferred_element_type=jnp.float32
     ).astype(jnp.bfloat16)
-    skeleton_charges = lax.all_gather(partial_value, "nbr", axis=2, tiled=True)
+    skeleton_charges = jnp.concatenate(
+        lax.all_to_all(jnp.stack([partial_value] * lax.axis_size("nbr")), "nbr", 0, 0), axis=2
+    )
     skeleton_points = jnp.take_along_axis(points, skeleton_index[:, None, :], axis=2)
     near_local, near_slots = slot_plan(near_ids, cap_near, groups, leaf_dev)
     far_local, far_slots = slot_plan(far_ids, cap_far, groups, leaf_dev)

time: 679 us -> 702 us (1.034)
  local copies, waits for them, and re-layouts: 246 us -> 259 us
    all_to_all x1, waiting for transfers between devices: 17 us -> 58.5 us  [per_device(): lax.all_to_all(skeleton_charges[far_wanted], 'leaf', split_axis=0, concat...]
    all_gather x1 -> x0, waiting for transfers between devices: 33.1 us -> none  [per_device(): skeleton_charges = lax.all_gather(partial_value, 'nbr', axis=2, tiled=True)]
    all_to_all x1, waiting for transfers between devices: 33.9 us -> 19.3 us  [per_device(): lax.all_to_all(points[near_wanted], 'leaf', split_axis=0, concat_axis=0,...]
    all_to_all x1, starting transfers between devices: 14 us -> 5.25 us  [per_device(): lax.all_to_all(skeleton_charges[far_wanted], 'leaf', split_axis=0, concat...]
    reshape x0 -> x2, local copies, waits for them, and re-layouts: none -> 8.33 us  [per_device(): jnp.concatenate(lax.all_to_all(jnp.stack([partial_value] * lax.axis_size(...]
    reduce_sum x8, other arithmetic: 0.45 us -> 7.66 us  [kernel_terms(): jnp.sum(target_f32 * target_f32, axis=0)[:, None]]
    unnamed x12 -> x16, local copies, waits for them, and re-layouts: 6.29 us -> 13.5 us
  transfers between devices with their start and end apart: 8 -> 8, of which waited for: 6 -> 6; matrix products, arithmetic and copies ran while one was open for 35% -> 36% of each run, Pallas kernels for 0% -> 0%
where the time goes in v1:
time: 702 us; the launch traced here: 692 us
  local copies, waits for them, and re-layouts  259 us (37%)
  waiting for transfers between devices  196 us (28%)
  matrix products  140 us (20%)
  starting transfers between devices  48.2 us (7%)
  other arithmetic  35.1 us (5%)
  between operations  13.9 us (2%)
    gather x1, local copies, waits for them, and re-layouts, per_device(): jnp.take_along_axis(points, skeleton_index[:, None, :], axis=2)  132 us
    dot_general x8, matrix products, kernel_terms(): jnp.einsum('rm,tm->rt', weights.astype(jnp.float32), kernel, precision=la...  109 us
    all_to_all x1, waiting for transfers between devices, per_device(): lax.all_to_all(skeleton_charges[far_wanted], 'leaf', split_axis=0, concat...  58.5 us
    reduce_scatter x1, waiting for transfers between devices, per_device(): return lax.psum_scatter(terms, 'nbr', scatter_dimension=2, tiled=True)  54.9 us
    all_to_all x1, waiting for transfers between devices, per_device(): lax.all_to_all(skeleton_points[far_wanted], 'leaf', split_axis=0, concat_...  31.1 us
    all_to_all x1, waiting for transfers between devices, per_device(): lax.all_to_all(charges[near_wanted], 'leaf', split_axis=0, concat_axis=0,...  30.5 us
    dot_general x8, matrix products, kernel_terms(): jnp.einsum('dt,dm->tm', targets, sources, preferred_element_type=jnp.floa...  27.9 us
    transpose x4, local copies, waits for them, and re-layouts, gather_entries(): picked.transpose(0, 2, 1, 3)  23.5 us
  transfers between devices with their start and end apart: 8, of which 6 were waited for; matrix products, arithmetic and copies ran while one was open for 36% of the time, Pallas kernels for 0%

profile of v1, /device:TPU:1, one launch (start us, length us, event | category | flops | bytes accessed | tf_op | source)
XLA Modules:
  0.0 692.3 jit_solution(3236454011176533825)
XLA Ops:
  8.8 8.6 %all-to-all-start = ((s32[32,1,3]{2,1,0:T(1,128)}), s32[32,1,3]{2,1,0:T(1,128)S(1)}, u32[]{:S(2)}, u32[]{:S(2)}) async-start(s32[32,1,3]{2,1,0:T(1,128)} %bitcast.4), calls=%async_computation | async-start | bytes 32768 | tf_op jit(solution)/shard_map/all_to_all | solution.py:91
  24.3 5.8 all-to-all-start.3
  40.5 132.5 %gather_fusion.8 = bf16[8192,32]{1,0:T(8,128)(2,1)} fusion(bf16[32,32,512]{1,2,0:T(8,128)(2,1)} %copy.60, s32[8192]{0:T(1024)S(1)} %bitcast.84), kind=kCustom, calls=%fused_computation.8 | custom fusion | bytes 1114112 | tf_op jit(solution)/shard_map/jit(take_along_axis)/gather | solution.py:85
  182.6 9.2 %gather_fusion.6 = bf16[160,32,256]{1,2,0:T(8,128)(2,1)} fusion(bf16[32,32,256]{1,2,0:T(8,128)(2,1)} %select_bitcast_fusion, s32[1024]{0:T(1024)S(1)} %pad_clamp_fusion.1), kind=kCustom, calls=%fused_computation.6 | custom fusion | bytes 5243520 | tf_op jit(solution)/shard_map/gather | solution.py:98
  191.8 9.8 %copy.61 = bf16[32,5,32,256]{3,2,1,0:T(8,128)(2,1)} copy(bf16[32,5,32,256]{2,3,1,0:T(8,128)(2,1)} %bitcast.90) | data formatting | bytes 5242880 | tf_op jit(solution)/shard_map/gather | solution.py:98
  201.6 7.6 %all-to-all-start.6 = ((bf16[32,5,32,256]{3,2,1,0:T(8,128)(2,1)}), bf16[32,5,32,256]{3,2,1,0:T(8,128)(2,1)}, u32[]{:S(2)}, u32[]{:S(2)}) async-start(bf16[32,5,32,256]{3,2,1,0:T(8,128)(2,1)} %copy.61), calls=%async_computation.6 | async-start | bytes 5242880 | tf_op jit(solution)/shard_map/all_to_all | solution.py:97
  212.1 31.1 %all-to-all-done.6 = bf16[32,5,32,256]{3,2,1,0:T(8,128)(2,1)} async-done(((bf16[32,5,32,256]{3,2,1,0:T(8,128)(2,1)}), bf16[32,5,32,256]{3,2,1,0:T(8,128)(2,1)}, u32[]{:S(2)}, u32[]{:S(2)}) %all-to-all-start.6) | async-done | bytes 2621472 | tf_op jit(solution)/shard_map/all_to_all | solution.py:97
  243.2 5.8 all-to-all-start.5
  261.6 7.7 %gather_fusion.2 = bf16[160,64,256]{2,1,0:T(8,128)(2,1)} fusion(bf16[32,64,256]{2,1,0:T(8,128)(2,1)S(1)} %reshape.413, s32[1024]{0:T(1024)S(1)} %pad_clamp_fusion.1), kind=kCustom, calls=%fused_computation.2 | custom fusion | bytes 10486400 | tf_op jit(solution)/shard_map/gather | solution.py:101
  269.3 19.3 %all-to-all-done.5 = bf16[32,3,32,512]{3,2,1,0:T(8,128)(2,1)} async-done(((bf16[32,3,32,512]{3,2,1,0:T(8,128)(2,1)}), bf16[32,3,32,512]{3,2,1,0:T(8,128)(2,1)}, u32[]{:S(2)}, u32[]{:S(2)}) %all-to-all-start.5) | async-done | bytes 3145760 | tf_op jit(solution)/shard_map/all_to_all | solution.py:95
  288.6 5.2 all-to-all-start.4
  293.9 6.0 gather_fusion
  299.9 58.5 %all-to-all-done.4 = bf16[32,5,64,256]{3,2,1,0:T(8,128)(2,1)} async-done(((bf16[32,5,64,256]{3,2,1,0:T(8,128)(2,1)}), bf16[32,5,64,256]{3,2,1,0:T(8,128)(2,1)}, u32[]{:S(2)}, u32[]{:S(2)}) %all-to-all-start.4) | async-done | bytes 5242912 | tf_op jit(solution)/shard_map/all_to_all | solution.py:100
  358.4 9.6 %all-to-all-start.1 = ((bf16[32,3,64,512]{3,2,1,0:T(8,128)(2,1)}), bf16[32,3,64,512]{3,2,1,0:T(8,128)(2,1)}, u32[]{:S(2)}, u32[]{:S(2)}) async-start(bf16[32,3,64,512]{3,2,1,0:T(8,128)(2,1)} %bitcast.86), calls=%async_computation.1 | async-start | bytes 12582912 | tf_op jit(solution)/shard_map/all_to_all | solution.py:96
  393.9 5.4 gather_fusion.3
  399.3 8.1 %copy.58 = bf16[32,64,4,256]{3,2,1,0:T(4,128)(2,1)} copy(bf16[32,64,4,256]{3,1,2,0:T(8,128)(2,1)} %bitcast.88) | data formatting | bytes 8388608 | tf_op jit(solution)/shard_map/transpose | solution.py:67
  407.4 7.9 %concatenate.17 = bf16[8,4,64,1024]{3,2,1,0:T(8,128)(2,1)} reshape(bf16[32,64,4,256]{3,2,1,0:T(4,128)(2,1)} %copy.58) | data formatting | bytes 8388608 | tf_op jit(solution)/shard_map/concatenate | solution.py:111
  415.3 30.5 %all-to-all-done.1 = bf16[32,3,64,512]{3,2,1,0:T(8,128)(2,1)} async-done(((bf16[32,3,64,512]{3,2,1,0:T(8,128)(2,1)}), bf16[32,3,64,512]{3,2,1,0:T(8,128)(2,1)}, u32[]{:S(2)}, u32[]{:S(2)}) %all-to-all-start.1) | async-done | bytes 6291488 | tf_op jit(solution)/shard_map/all_to_all | solution.py:96
  445.8 5.6 gather_fusion.1
  451.4 8.5 %copy.53 = bf16[32,64,2,512]{3,2,1,0:T(2,128)(2,1)} copy(bf16[32,64,2,512]{3,1,2,0:T(8,128)(2,1)} %bitcast.89) | data formatting | bytes 8388608 | tf_op jit(solution)/shard_map/transpose | solution.py:67
  459.9 7.8 %concatenate.16 = bf16[8,4,64,1024]{3,2,1,0:T(8,128)(2,1)} reshape(bf16[32,64,2,512]{3,2,1,0:T(2,128)(2,1)} %copy.53) | data formatting | bytes 8388608 | tf_op jit(solution)/shard_map/concatenate | solution.py:111
  467.6 8.2 %pad_maximum_fusion = bf16[8,4,64,2048]{3,2,1,0:T(8,128)(2,1)} fusion(bf16[8,4,64,1024]{3,2,1,0:T(8,128)(2,1)} %concatenate.17, bf16[8,4,64,1024]{3,2,1,0:T(8,128)(2,1)} %concatenate.16), kind=kLoop, calls=%fused_computation.34 | loop fusion | flops 16777216 | bytes 16777216 | tf_op jit(solution)/shard_map/concatenate | solution.py:111
  475.8 154.6 %while.10 = (s32[]{:T(128)}, f32[8,4,64,512]{3,2,1,0:T(8,128)}, bf16[8,4,64,2048]{3,2,1,0:T(8,128)(2,1)}, bf16[8,4,32,512]{3,2,1,0:T(8,128)(2,1)}, bf16[8,4,32,2048]{3,2,1,0:T(8,128)(2,1)}, /*index=5*/s32[]{:T(128)}) while((s32[]{:T(128)}, f32[8,4,64,512]{3,2,1,0:T(8,128)}, bf16[8,4,64,2048]{3,2,1,0:T(8,128)(2,1)}, ...), condition=%wide.region_9.10_spmd, body=%wide.region_6.9_spmd.sunk | while | flops 3507410944 | bytes 36522060 | solution.py:43
  481.6 13.6 %fusion.45 = f32[8,4,64,512]{3,2,1,0:T(8,128)} fusion(f32[8,4,64,512]{3,2,1,0:T(8,128)} %get-tuple-element.85, s32[]{:T(128)} %get-tuple-element.84, f32[4,512,2048]{2,1,0:T(8,128)S(1)} %fusion.44, f32[4,2048]{1,0:T(4,128)S(1)} %multiply_reduce_fusion.4, f32[4,512]{1,0:T(4,128)S(1)} %multiply_reduce_fusion.5, ...), kind=kOutput, calls=%fused_computation.20.clone.1 | convolution fusion | flops 3238002688 | bytes 18392064 | tf_op jit(solution)/shard_map/while/body/eval_jaxpr/vmap(rm,tm->rt)/dot_general | solution.py:20
  501.0 13.6 %fusion.45 = f32[8,4,64,512]{3,2,1,0:T(8,128)} fusion(f32[8,4,64,512]{3,2,1,0:T(8,128)} %get-tuple-element.85, s32[]{:T(128)} %get-tuple-element.84, f32[4,512,2048]{2,1,0:T(8,128)S(1)} %fusion.44, f32[4,2048]{1,0:T(4,128)S(1)} %multiply_reduce_fusion.4, f32[4,512]{1,0:T(4,128)S(1)} %multiply_reduce_fusion.5, ...), kind=kOutput, calls=%fused_computation.20.clone.1 | convolution fusion | flops 3238002688 | bytes 18392064 | tf_op jit(solution)/shard_map/while/body/eval_jaxpr/vmap(rm,tm->rt)/dot_general | solution.py:20
  520.2 13.6 %fusion.45 = f32[8,4,64,512]{3,2,1,0:T(8,128)} fusion(f32[8,4,64,512]{3,2,1,0:T(8,128)} %get-tuple-element.85, s32[]{:T(128)} %get-tuple-element.84, f32[4,512,2048]{2,1,0:T(8,128)S(1)} %fusion.44, f32[4,2048]{1,0:T(4,128)S(1)} %multiply_reduce_fusion.4, f32[4,512]{1,0:T(4,128)S(1)} %multiply_reduce_fusion.5, ...), kind=kOutput, calls=%fused_computation.20.clone.1 | convolution fusion | flops 3238002688 | bytes 18392064 | tf_op jit(solution)/shard_map/while/body/eval_jaxpr/vmap(rm,tm->rt)/dot_general | solution.py:20
  539.5 13.6 %fusion.45 = f32[8,4,64,512]{3,2,1,0:T(8,128)} fusion(f32[8,4,64,512]{3,2,1,0:T(8,128)} %get-tuple-element.85, s32[]{:T(128)} %get-tuple-element.84, f32[4,512,2048]{2,1,0:T(8,128)S(1)} %fusion.44, f32[4,2048]{1,0:T(4,128)S(1)} %multiply_reduce_fusion.4, f32[4,512]{1,0:T(4,128)S(1)} %multiply_reduce_fusion.5, ...), kind=kOutput, calls=%fused_computation.20.clone.1 | convolution fusion | flops 3238002688 | bytes 18392064 | tf_op jit(solution)/shard_map/while/body/eval_jaxpr/vmap(rm,tm->rt)/dot_general | solution.py:20
  558.8 13.6 %fusion.45 = f32[8,4,64,512]{3,2,1,0:T(8,128)} fusion(f32[8,4,64,512]{3,2,1,0:T(8,128)} %get-tuple-element.85, s32[]{:T(128)} %get-tuple-element.84, f32[4,512,2048]{2,1,0:T(8,128)S(1)} %fusion.44, f32[4,2048]{1,0:T(4,128)S(1)} %multiply_reduce_fusion.4, f32[4,512]{1,0:T(4,128)S(1)} %multiply_reduce_fusion.5, ...), kind=kOutput, calls=%fused_computation.20.clone.1 | convolution fusion | flops 3238002688 | bytes 18392064 | tf_op jit(solution)/shard_map/while/body/eval_jaxpr/vmap(rm,tm->rt)/dot_general | solution.py:20
  578.1 13.6 %fusion.45 = f32[8,4,64,512]{3,2,1,0:T(8,128)} fusion(f32[8,4,64,512]{3,2,1,0:T(8,128)} %get-tuple-element.85, s32[]{:T(128)} %get-tuple-element.84, f32[4,512,2048]{2,1,0:T(8,128)S(1)} %fusion.44, f32[4,2048]{1,0:T(4,128)S(1)} %multiply_reduce_fusion.4, f32[4,512]{1,0:T(4,128)S(1)} %multiply_reduce_fusion.5, ...), kind=kOutput, calls=%fused_computation.20.clone.1 | convolution fusion | flops 3238002688 | bytes 18392064 | tf_op jit(solution)/shard_map/while/body/eval_jaxpr/vmap(rm,tm->rt)/dot_general | solution.py:20
  597.4 13.6 %fusion.45 = f32[8,4,64,512]{3,2,1,0:T(8,128)} fusion(f32[8,4,64,512]{3,2,1,0:T(8,128)} %get-tuple-element.85, s32[]{:T(128)} %get-tuple-element.84, f32[4,512,2048]{2,1,0:T(8,128)S(1)} %fusion.44, f32[4,2048]{1,0:T(4,128)S(1)} %multiply_reduce_fusion.4, f32[4,512]{1,0:T(4,128)S(1)} %multiply_reduce_fusion.5, ...), kind=kOutput, calls=%fused_computation.20.clone.1 | convolution fusion | flops 3238002688 | bytes 18392064 | tf_op jit(solution)/shard_map/while/body/eval_jaxpr/vmap(rm,tm->rt)/dot_general | solution.py:20
  616.7 13.6 %fusion.45 = f32[8,4,64,512]{3,2,1,0:T(8,128)} fusion(f32[8,4,64,512]{3,2,1,0:T(8,128)} %get-tuple-element.85, s32[]{:T(128)} %get-tuple-element.84, f32[4,512,2048]{2,1,0:T(8,128)S(1)} %fusion.44, f32[4,2048]{1,0:T(4,128)S(1)} %multiply_reduce_fusion.4, f32[4,512]{1,0:T(4,128)S(1)} %multiply_reduce_fusion.5, ...), kind=kOutput, calls=%fused_computation.20.clone.1 | convolution fusion | flops 3238002688 | bytes 18392064 | tf_op jit(solution)/shard_map/while/body/eval_jaxpr/vmap(rm,tm->rt)/dot_general | solution.py:20
  630.4 54.9 %reduce-scatter.2.cloned.1.call-done = f32[32,64,128]{2,1,0:T(8,128)} async-done(((f32[32,64,512]{2,1,0:T(8,128)}), f32[32,64,128]{2,1,0:T(8,128)}) %reduce-scatter.2.cloned.1.call-update) | async-done | bytes 1048592 | tf_op jit(solution)/shard_map/reduce_scatter | solution.py:119
  (92 shorter events, 115.7 us)
Async XLA Ops:
  6.5 12.1 %copy-start = (bf16[32,64,512]{2,1,0:T(8,128)(2,1)S(1)}, bf16[32,64,512]{2,1,0:T(8,128)(2,1)}, u32[]{:S(2)}) copy-start(bf16[32,64,512]{2,1,0:T(8,128)(2,1)} %param.9) | copy-start | bytes 6291460
  6.5 23.5 %copy-start.4 = (s32[32,256]{1,0:T(8,128)S(1)}, s32[32,256]{1,0:T(8,128)}, u32[]{:S(2)}) copy-start(s32[32,256]{1,0:T(8,128)} %param.11) | copy-start | bytes 98308
  8.8 15.6 %all-to-all-start = ((s32[32,1,3]{2,1,0:T(1,128)}), s32[32,1,3]{2,1,0:T(1,128)S(1)}, u32[]{:S(2)}, u32[]{:S(2)}) async-start(s32[32,1,3]{2,1,0:T(1,128)} %bitcast.4), calls=%async_computation | async-start | bytes 32768 | tf_op jit(solution)/shard_map/all_to_all | solution.py:91
  18.7 18.7 %copy-start.2 = (bf16[32,32,512]{2,1,0:T(8,128)(2,1)S(1)}, bf16[32,32,512]{2,1,0:T(8,128)(2,1)}, u32[]{:S(2)}) copy-start(bf16[32,32,512]{2,1,0:T(8,128)(2,1)} %param.8) | copy-start | bytes 3145732
  24.3 148.7 %all-to-all-start.3 = ((s32[32,1,5]{2,1,0:T(1,128)}), s32[32,1,5]{2,1,0:T(1,128)S(1)}, u32[]{:S(2)}, u32[]{:S(2)}) async-start(s32[32,1,5]{2,1,0:T(1,128)} %bitcast.13), calls=%async_computation.3 | async-start | bytes 32768 | tf_op jit(solution)/shard_map/all_to_all | solution.py:92
  173.0 28.6 %all-to-all-start.2 = ((bf16[4,2,65536]{2,1,0:T(2,128)(2,1)}), bf16[4,2,65536]{2,1,0:T(2,128)(2,1)}, u32[]{:S(2)}, u32[]{:S(2)}) async-start(bf16[4,2,65536]{2,1,0:T(2,128)(2,1)} %reshape.504), calls=%async_computation.2 | async-start | bytes 2097152 | tf_op jit(solution)/shard_map/all_to_all | solution.py:83
  201.6 41.6 %all-to-all-start.6 = ((bf16[32,5,32,256]{3,2,1,0:T(8,128)(2,1)}), bf16[32,5,32,256]{3,2,1,0:T(8,128)(2,1)}, u32[]{:S(2)}, u32[]{:S(2)}) async-start(bf16[32,5,32,256]{3,2,1,0:T(8,128)(2,1)} %copy.61), calls=%async_computation.6 | async-start | bytes 5242880 | tf_op jit(solution)/shard_map/all_to_all | solution.py:97
  243.2 45.4 %all-to-all-start.5 = ((bf16[32,3,32,512]{3,2,1,0:T(8,128)(2,1)}), bf16[32,3,32,512]{3,2,1,0:T(8,128)(2,1)}, u32[]{:S(2)}, u32[]{:S(2)}) async-start(bf16[32,3,32,512]{3,2,1,0:T(8,128)(2,1)} %bitcast.91), calls=%async_computation.5 | async-start | bytes 6291456 | tf_op jit(solution)/shard_map/all_to_all | solution.py:95
  288.6 69.8 %all-to-all-start.4 = ((bf16[32,5,64,256]{3,2,1,0:T(8,128)(2,1)}), bf16[32,5,64,256]{3,2,1,0:T(8,128)(2,1)}, u32[]{:S(2)}, u32[]{:S(2)}) async-start(bf16[32,5,64,256]{3,2,1,0:T(8,128)(2,1)} %bitcast.87), calls=%async_computation.4 | async-start | bytes 10485760 | tf_op jit(solution)/shard_map/all_to_all | solution.py:100
  358.4 87.4 %all-to-all-start.1 = ((bf16[32,3,64,512]{3,2,1,0:T(8,128)(2,1)}), bf16[32,3,64,512]{3,2,1,0:T(8,128)(2,1)}, u32[]{:S(2)}, u32[]{:S(2)}) async-start(bf16[32,3,64,512]{3,2,1,0:T(8,128)(2,1)} %bitcast.86), calls=%async_computation.1 | async-start | bytes 12582912 | tf_op jit(solution)/shard_map/all_to_all | solution.py:96
  368.0 317.2 %reduce-scatter.2.cloned.1.call-start = ((), (), s32[]{:S(2)}) async-start(), calls=%async_computation.8 | async-start | bytes 5242880 | tf_op jit(solution)/shard_map/reduce_scatter | solution.py:119
  385.2 4.6 copy-start.3
  630.3 54.9 %copy-start.1 = (bf16[32,64,512]{2,1,0:T(8,128)(2,1)S(1)}, bf16[32,64,512]{2,1,0:T(8,128)(2,1)}, u32[]{:S(2)}) copy-start(bf16[32,64,512]{2,1,0:T(8,128)(2,1)} %param.9) | copy-start | bytes 6291460
Sparse Core Ops, SparseCore 0:
  630.5 54.7 reduce-scatter.1
